TPU v7x, 256 devices: a whole 4x4x8 slice. The times are simulated.
256 devices in a mesh: paths: 8 (over x, core), cpty: 32 (over z, y).
Axes of the slice: x: 4, y: 4, z: 8, core: 2. Of those that a mesh axis runs over, the one named last changes fastest.
Arguments:
- factors: bfloat16 [64, 12288], P(None, 'paths'), may hold values from -6 to 6
- loadings: bfloat16 [64, 65536], P(None, 'cpty'), may hold values from -2 to 2
- notional: bfloat16 [65536], P('cpty'), may hold values from 0.25 to 0.796875
- strike: bfloat16 [65536], P('cpty'), may hold values from 2 to 8
- curvature: bfloat16 [65536], P('cpty'), may hold values from 1 to 3
- trade_cpty: int32 [65536], P('cpty'), may hold values from 0 to 4095, as said below
Outputs:
- exposure: bfloat16 [12288, 4096], P('paths', 'cpty')
- moment: float32 [4096, 4096], P('paths', 'cpty')
Inputs may be any that keep to these rules, and one draw needn't show every extreme that they name: `trade_cpty`: of the trades in the book of one index of cpty, at most 128 belong to the counterparties numbered k * 128 to (k + 1) * 128 - 1 for any k; in every draw some such k receives exactly 128 from every book.
All inputs are finite; a program needn't handle non-finite values.
Results may differ from a plain program's by a relative error of at most 0.0064.
Values may be sent and summed in bfloat16 or wider, within the bound.
A program may use at most 128 MiB of HBM per device.

v0:
```python
import jax
import jax.numpy as jnp
from jax import lax
from jax.sharding import PartitionSpec as P

CP_DEV = 128


def in_blocks(x, dim, length):
    before, after = (x.shape[:dim], x.shape[dim + 1 :])
    return jnp.moveaxis(x.reshape(*before, length, -1, *after), dim, 0)


def summed_on_arrival(x, axis, dim):
    parts = in_blocks(x, dim, lax.axis_size(axis))
    arrived = lax.all_to_all(parts, axis, split_axis=0, concat_axis=0, tiled=True)
    return arrived.astype(jnp.float32).sum(axis=0)


def price_trades(drivers, loading_cols, trade_terms):
    linear = jnp.dot(drivers, loading_cols, preferred_element_type=jnp.float32)
    terms_wide = trade_terms.astype(jnp.float32)
    value = terms_wide[0] * (linear + terms_wide[2] * jnp.tanh(linear - terms_wide[1]))
    return value.astype(jnp.bfloat16)


def on_device(factors, loadings, notional, strike, curvature, trade_cpty):
    groups = lax.axis_size("cpty")
    own_index = lax.axis_index("cpty")
    trades = loadings.shape[1]
    slot_size = 2 * trades // groups
    owners = trade_cpty // CP_DEV
    marked = (owners[:, None] == jnp.arange(groups, dtype=jnp.int32)[None, :]).astype(jnp.int32)
    ranking = jnp.sum((jnp.cumsum(marked, axis=0) - marked) * marked, axis=1)
    target = owners * slot_size + ranking
    chosen = (
        jnp.zeros((groups * slot_size,), jnp.int32)
        .at[target]
        .set(jnp.arange(trades, dtype=jnp.int32))
    )
    filled = jnp.zeros((groups * slot_size,), jnp.bool_).at[target].set(True)
    labels = jnp.where(filled, trade_cpty[chosen], -1)[None, :]
    drivers = jnp.transpose(factors)
    trade_terms = jnp.stack([notional, strike, curvature])
    described = jnp.concatenate([loadings, trade_terms], axis=0)
    packed = jnp.where(
        filled[None, :], jnp.take(described, chosen, axis=1), jnp.zeros((), jnp.bfloat16)
    )
    received, arrived_ids = (
        lax.all_to_all(packed, "cpty", split_axis=1, concat_axis=1, tiled=True),
        lax.all_to_all(labels, "cpty", split_axis=1, concat_axis=1, tiled=True),
    )
    factor_count = loadings.shape[0]
    arrived = price_trades(drivers, received[:factor_count], received[factor_count:])
    local_ids = arrived_ids[0] - own_index * CP_DEV
    onehot = (local_ids[:, None] == jnp.arange(CP_DEV, dtype=jnp.int32)[None, :]).astype(
        jnp.bfloat16
    )
    netted = jnp.dot(arrived, onehot, preferred_element_type=jnp.float32)
    exposure = jnp.maximum(netted, 0.0).astype(jnp.bfloat16)
    everyone = lax.all_gather(exposure, "cpty", axis=1, tiled=True)
    path_total = exposure.shape[0] * lax.axis_size("paths")
    moment = (
        summed_on_arrival(
            jnp.einsum("pa,pb->ab", everyone, exposure, preferred_element_type=jnp.float32).astype(
                jnp.bfloat16
            ),
            "paths",
            0,
        )
        / path_total
    )
    return (exposure, moment)


def solution(mesh):
    in_specs = (P(None, "paths"), P(None, "cpty"), P("cpty"), P("cpty"), P("cpty"), P("cpty"))
    out_specs = (P("paths", "cpty"), P("paths", "cpty"))
    return jax.shard_map(
        on_device, mesh=mesh, in_specs=in_specs, out_specs=out_specs, check_vma=False
    )
```

profile of v0, /device:TPU:1, one launch (start us, length us, event | category | flops | bytes accessed | tf_op | source)
XLA Modules:
  0.0 287.2 jit_solution(17059434159926769436)
XLA Ops:
  7.2 0.8 add_select_fusion
  8.0 9.1 %reduce-window.6 = s32[32,16,128]{2,1,0:T(8,128)S(1)} reduce-window(s32[32,16,128]{2,1,0:T(8,128)S(1)} %fusion.18, s32[]{:T(128)} %constant.24.clone.1), window={size=1x1x128 pad=0_0x0_0x127_0}, to_apply=%region_0.1 | reduce-window | flops 8323072 | bytes 524292 | tf_op jit(solution)/shard_map/reduce-window
  17.1 0.1 slice.40
  17.2 0.2 copy.33
  17.5 0.2 reduce-window.9
  17.7 0.1 broadcast_add_fusion
  17.8 0.1 fusion.17
  17.9 0.7 compare_select_fusion.1
  18.7 8.1 %scatter_custom_fusion.1 = s32[4096]{0:T(1024)S(1)} fusion(s32[2048]{0:T(1024)S(1)} %compare_select_fusion.1, s32[2048]{0:T(1024)S(1)} %iota.15, s32[]{:T(128)} %constant.24.clone.1), kind=kCustom, calls=%fused_computation.49 | custom fusion | bytes 16388 | tf_op jit(solution)/shard_map/scatter | solution.py:39
  26.7 23.0 %gather_fusion.1 = s32[4096]{0:T(1024)S(1)} fusion(s32[2048]{0:T(1024)S(1)} %copy-done.1, s32[4096]{0:T(1024)S(1)} %fusion.19), kind=kCustom, calls=%fused_computation.1 | custom fusion | bytes 49152 | tf_op jit(solution)/shard_map/gather | solution.py:42
  49.8 9.1 %scatter_custom_fusion = pred[4096]{0:T(1024)(128)(4,1)S(1)} fusion(s32[2048]{0:T(1024)S(1)} %compare_select_fusion.1, pred[2048]{0:T(1024)(128)(4,1)S(1)} %broadcast.49, pred[]{:T(512)} %constant.22.clone.1), kind=kCustom, calls=%fused_computation.53 | custom fusion | bytes 4097 | tf_op jit(solution)/shard_map/scatter | solution.py:41
  58.9 0.6 broadcast_select_fusion
  59.5 12.0 %all-to-all-start.1 = ((s32[1,32,128]{2,0,1:T(1,128)}), s32[1,32,128]{2,0,1:T(1,128)S(1)}, u32[]{:S(2)}, u32[]{:S(2)}) async-start(s32[1,32,128]{2,0,1:T(1,128)} %bitcast.12), calls=%async_computation.1 | async-start | bytes 32768 | tf_op jit(solution)/shard_map/all_to_all | solution.py:51
  71.6 0.3 copy.26
  71.9 0.3 stack.12
  72.3 0.3 stack.13
  72.6 0.3 stack.14
  72.9 0.7 pad_maximum_fusion
  73.7 12.1 %gather_fusion = bf16[4096,67]{1,0:T(8,128)(2,1)S(1)} fusion(bf16[67,2048]{0,1:T(8,128)(2,1)S(1)} %pad_maximum_fusion, s32[4096]{0:T(1024)S(1)} %fusion.19), kind=kCustom, calls=%fused_computation | custom fusion | bytes 1114112 | tf_op jit(solution)/shard_map/jit(_take)/gather | solution.py:47
  85.8 0.6 copy.30
  86.4 0.9 select_select_fusion
  87.3 9.2 %all-to-all-start = ((bf16[67,32,128]{2,0,1:T(8,128)(2,1)}), bf16[67,32,128]{2,0,1:T(8,128)(2,1)S(1)}, u32[]{:S(2)}, u32[]{:S(2)}) async-start(bf16[67,32,128]{2,0,1:T(8,128)(2,1)} %select_select_fusion), calls=%async_computation | async-start | bytes 1179648 | tf_op jit(solution)/shard_map/all_to_all | solution.py:50
  96.6 0.0 all-gather.2.cloned.1.call-start
  96.6 0.9 iota_compare_fusion.7
  97.5 15.6 %all-to-all-done = bf16[67,32,128]{2,0,1:T(8,128)(2,1)S(1)} async-done(((bf16[67,32,128]{2,0,1:T(8,128)(2,1)}), bf16[67,32,128]{2,0,1:T(8,128)(2,1)S(1)}, u32[]{:S(2)}, u32[]{:S(2)}) %all-to-all-start) | async-done | bytes 548896 | tf_op jit(solution)/shard_map/all_to_all | solution.py:50
  113.2 14.0 %fusion.9 = bf16[1536,128]{1,0:T(8,128)(2,1)} fusion(bf16[64,1536]{1,0:T(8,128)(2,1)S(1)} %copy-done, f32[4096]{0:T(1024)S(1)} %get-tuple-element.3, f32[4096]{0:T(1024)S(1)} %get-tuple-element.4, f32[4096]{0:T(1024)S(1)} %get-tuple-element.2, bf16[67,32,128]{2,0,1:T(8,128)(2,1)S(1)} %all-to-all-done, pred[4096,128]{1,0:T(32,128)(4,1)S(1)} %iota_compare_fusion.7), kind=kOutput, calls=%fused_computation.16 | convolution fusion | flops 2447769600 | bytes 1687552 | tf_op jit(solution)/shard_map/dot_general | solution.py:59
  127.2 0.0 all-gather.2.cloned.1.call-update
  127.2 121.3 %all-gather.2.cloned.1.call-done = bf16[1536,4096]{1,0:T(8,128)(2,1)} async-done(((bf16[1536,128]{1,0:T(8,128)(2,1)}), bf16[1536,4096]{1,0:T(8,128)(2,1)}) %all-gather.2.cloned.1.call-update) | async-done | bytes 12582928 | tf_op jit(solution)/shard_map/all_gather | solution.py:61
  248.5 8.1 %convolution_convert_fusion = bf16[4096,128]{1,0:T(8,128)(2,1)S(1)} fusion(bf16[1536,4096]{1,0:T(8,128)(2,1)} %all-gather.2.cloned.1.call-done, bf16[1536,128]{1,0:T(8,128)(2,1)} %fusion.9), kind=kOutput, calls=%fused_computation.14 | convolution fusion | flops 1611137024 | bytes 14024704 | tf_op jit(solution)/shard_map/pa,pb->ab/dot_general | solution.py:65
  256.5 23.0 %all_to_all.20 = bf16[8,512,128]{2,1,0:T(8,128)(2,1)S(1)} all-to-all(bf16[8,512,128]{2,1,0:T(8,128)(2,1)S(1)} %bitcast.86), channel_id=1, replica_groups=mesh['paths'=8,'cpty'=32] {'paths'}, dimensions={0} | all-to-all | bytes 2097152 | tf_op jit(solution)/shard_map/all_to_all | solution.py:16
  279.5 0.1 convert_reduce_fusion
  279.6 0.7 broadcast_multiply_fusion
  (22 shorter events, 0.1 us)
Async XLA Ops:
  7.2 106.0 %copy-start = (bf16[64,1536]{1,0:T(8,128)(2,1)S(1)}, bf16[64,1536]{1,0:T(8,128)(2,1)}, u32[]{:S(2)}) copy-start(bf16[64,1536]{1,0:T(8,128)(2,1)} %param.6) | copy-start | bytes 589828
  7.2 19.6 %copy-start.1 = (s32[2048]{0:T(1024)S(1)}, s32[2048]{0:T(1024)}, u32[]{:S(2)}) copy-start(s32[2048]{0:T(1024)} %param.11) | copy-start | bytes 24580
  7.2 64.4 %copy-start.2 = (bf16[64,2048]{1,0:T(8,128)(2,1)S(1)}, bf16[64,2048]{1,0:T(8,128)(2,1)}, u32[]{:S(2)}) copy-start(bf16[64,2048]{1,0:T(8,128)(2,1)} %param.7) | copy-start | bytes 786436
  7.2 64.7 %copy-start.3 = (bf16[2048]{0:T(1024)(128)(2,1)S(1)}, bf16[2048]{0:T(1024)(128)(2,1)}, u32[]{:S(2)}) copy-start(bf16[2048]{0:T(1024)(128)(2,1)} %param.8) | copy-start | bytes 12292
  7.2 65.0 %copy-start.4 = (bf16[2048]{0:T(1024)(128)(2,1)S(1)}, bf16[2048]{0:T(1024)(128)(2,1)}, u32[]{:S(2)}) copy-start(bf16[2048]{0:T(1024)(128)(2,1)} %param.9) | copy-start | bytes 12292
  7.2 65.4 %copy-start.5 = (bf16[2048]{0:T(1024)(128)(2,1)S(1)}, bf16[2048]{0:T(1024)(128)(2,1)}, u32[]{:S(2)}) copy-start(bf16[2048]{0:T(1024)(128)(2,1)} %param.10) | copy-start | bytes 12292
  59.5 27.8 %all-to-all-start.1 = ((s32[1,32,128]{2,0,1:T(1,128)}), s32[1,32,128]{2,0,1:T(1,128)S(1)}, u32[]{:S(2)}, u32[]{:S(2)}) async-start(s32[1,32,128]{2,0,1:T(1,128)} %bitcast.12), calls=%async_computation.1 | async-start | bytes 32768 | tf_op jit(solution)/shard_map/all_to_all | solution.py:51
  87.3 25.8 %all-to-all-start = ((bf16[67,32,128]{2,0,1:T(8,128)(2,1)}), bf16[67,32,128]{2,0,1:T(8,128)(2,1)S(1)}, u32[]{:S(2)}, u32[]{:S(2)}) async-start(bf16[67,32,128]{2,0,1:T(8,128)(2,1)} %select_select_fusion), calls=%async_computation | async-start | bytes 1179648 | tf_op jit(solution)/shard_map/all_to_all | solution.py:50
  96.6 151.9 %all-gather.2.cloned.1.call-start = ((), (), s32[]{:S(2)}) async-start(), calls=%async_computation.3 | async-start | bytes 12976128 | tf_op jit(solution)/shard_map/all_gather | solution.py:61
Sparse Core Ops, SparseCore 0:
  127.3 121.1 all-gather.1
where the time goes:
time: 288 us; the launch traced here: 287 us
  waiting for transfers between devices  137 us (48%)
  local copies, waits for them, and re-layouts  54.7 us (19%)
  blocking collectives  23 us (8%)
  matrix products  22.1 us (8%)
  starting transfers between devices  21.3 us (7%)
  other arithmetic  15 us (5%)
  between operations  14.3 us (5%)
    all_gather x1, waiting for transfers between devices, on_device(): everyone = lax.all_gather(exposure, 'cpty', axis=1, tiled=True)  121 us
    gather x1, local copies, waits for them, and re-layouts, on_device(): labels = jnp.where(filled, trade_cpty[chosen], -1)[None, :]  23 us
    all_to_all x1, blocking collectives, summed_on_arrival(): lax.all_to_all(parts, axis, split_axis=0, concat_axis=0, tiled=True)  23 us
    all_to_all x1, waiting for transfers between devices, on_device(): lax.all_to_all(packed, 'cpty', split_axis=1, concat_axis=1, tiled=True)  15.6 us
    dot_general x1, matrix products, on_device(): netted = jnp.dot(arrived, onehot, preferred_element_type=jnp.float32)  14 us
    gather x2, local copies, waits for them, and re-layouts, on_device(): jnp.take(described, chosen, axis=1)  12.8 us
    all_to_all x1, starting transfers between devices, on_device(): lax.all_to_all(labels, 'cpty', split_axis=1, concat_axis=1, tiled=True)  12 us
    another operation x3, other arithmetic  9.41 us
  transfers between devices with their start and end apart: 3, of which 2 were waited for; matrix products, arithmetic and copies ran while one was open for 6% of the time, Pallas kernels for 0%

commit v1 on v0

--- a/solution.py
+++ b/solution.py
@@ -58,7 +58,9 @@
     )
     netted = jnp.dot(arrived, onehot, preferred_element_type=jnp.float32)
     exposure = jnp.maximum(netted, 0.0).astype(jnp.bfloat16)
-    everyone = lax.all_gather(exposure, "cpty", axis=1, tiled=True)
+    everyone = jnp.concatenate(
+        lax.all_to_all(jnp.stack([exposure] * lax.axis_size("cpty")), "cpty", 0, 0), axis=1
+    )
     path_total = exposure.shape[0] * lax.axis_size("paths")
     moment = (
         summed_on_arrival(

time: 288 us -> 432 us (1.50)
  blocking collectives: 23 us -> 302 us
  waiting for transfers between devices: 137 us -> 15.6 us
  between operations: 14.3 us -> 0.93 us
  local copies, waits for them, and re-layouts: 54.7 us -> 60.8 us
  matrix products: 22.1 us -> 16.8 us
    all_to_all x0 -> x1, blocking collectives: none -> 279 us  [on_device(): lax.all_to_all(jnp.stack([exposure] * lax.axis_size('cpty')), 'cpty', 0, 0)]
    all_gather x1 -> x0, waiting for transfers between devices: 121 us -> none  [on_device(): everyone = lax.all_gather(exposure, 'cpty', axis=1, tiled=True)]
    another operation x1 -> x2, local copies, waits for them, and re-layouts: 0.24 us -> 6.22 us  [the longest x1 5.99 us: on_device(): jnp.stack([exposure] * lax.axis_size('cpty'))]
    dot_general x1, matrix products: 8.06 us -> 3.61 us  [on_device(): jnp.einsum('pa,pb->ab', everyone, exposure, preferred_element_type=jnp.fl...]
  transfers between devices with their start and end apart: 3 -> 2, of which waited for: 2 -> 1; matrix products, arithmetic and copies ran while one was open for 6% -> 4% of each run, Pallas kernels for 0% -> 0%
where the time goes in v1:
time: 432 us
  blocking collectives  302 us (70%)
  local copies, waits for them, and re-layouts  60.8 us (14%)
  starting transfers between devices  21.2 us (5%)
  matrix products  16.8 us (4%)
  waiting for transfers between devices  15.6 us (4%)
  other arithmetic  15 us (3%)
    all_to_all x1, blocking collectives, on_device(): lax.all_to_all(jnp.stack([exposure] * lax.axis_size('cpty')), 'cpty', 0, 0)  279 us
    gather x1, local copies, waits for them, and re-layouts, on_device(): labels = jnp.where(filled, trade_cpty[chosen], -1)[None, :]  23 us
    all_to_all x1, blocking collectives, summed_on_arrival(): lax.all_to_all(parts, axis, split_axis=0, concat_axis=0, tiled=True)  22.4 us
    all_to_all x1, waiting for transfers between devices, on_device(): lax.all_to_all(packed, 'cpty', split_axis=1, concat_axis=1, tiled=True)  15.6 us
    dot_general x1, matrix products, on_device(): netted = jnp.dot(arrived, onehot, preferred_element_type=jnp.float32)  13.2 us
    gather x2, local copies, waits for them, and re-layouts, on_device(): jnp.take(described, chosen, axis=1)  12.7 us
    all_to_all x1, starting transfers between devices, on_device(): lax.all_to_all(labels, 'cpty', split_axis=1, concat_axis=1, tiled=True)  12 us
    another operation x3, other arithmetic  9.41 us
  transfers between devices with their start and end apart: 2, of which 1 were waited for; matrix products, arithmetic and copies ran while one was open for 4% of the time, Pallas kernels for 0%

profile of v1, /device:TPU:1, one launch (start us, length us, event | category | flops | bytes accessed | tf_op | source)
XLA Modules:
  0.0 432.0 jit_solution(14511910691201038168)
XLA Ops:
  0.7 0.8 add_select_fusion
  1.5 9.1 %reduce-window.6 = s32[32,16,128]{2,1,0:T(8,128)S(1)} reduce-window(s32[32,16,128]{2,1,0:T(8,128)S(1)} %fusion.18, s32[]{:T(128)} %constant.24.clone.1), window={size=1x1x128 pad=0_0x0_0x127_0}, to_apply=%region_0.1 | reduce-window | flops 8323072 | bytes 524292 | tf_op jit(solution)/shard_map/reduce-window
  10.6 0.1 slice.40
  10.7 0.2 copy.36
  11.0 0.2 reduce-window.9
  11.1 0.1 broadcast_add_fusion
  11.3 0.1 fusion.17
  11.4 0.7 compare_select_fusion.1
  12.1 8.1 %scatter_custom_fusion.1 = s32[4096]{0:T(1024)S(1)} fusion(s32[2048]{0:T(1024)S(1)} %compare_select_fusion.1, s32[2048]{0:T(1024)S(1)} %iota.15, s32[]{:T(128)} %constant.24.clone.1), kind=kCustom, calls=%fused_computation.49 | custom fusion | bytes 16388 | tf_op jit(solution)/shard_map/scatter | solution.py:39
  20.2 23.0 %gather_fusion.1 = s32[4096]{0:T(1024)S(1)} fusion(s32[2048]{0:T(1024)S(1)} %copy-done.1, s32[4096]{0:T(1024)S(1)} %fusion.19), kind=kCustom, calls=%fused_computation.1 | custom fusion | bytes 49152 | tf_op jit(solution)/shard_map/gather | solution.py:42
  43.3 9.1 %scatter_custom_fusion = pred[4096]{0:T(1024)(128)(4,1)S(1)} fusion(s32[2048]{0:T(1024)S(1)} %compare_select_fusion.1, pred[2048]{0:T(1024)(128)(4,1)S(1)} %broadcast.51, pred[]{:T(512)} %constant.22.clone.1), kind=kCustom, calls=%fused_computation.53 | custom fusion | bytes 4097 | tf_op jit(solution)/shard_map/scatter | solution.py:41
  52.4 0.6 broadcast_select_fusion
  53.0 12.0 %all-to-all-start.1 = ((s32[1,32,128]{2,0,1:T(1,128)}), s32[1,32,128]{2,0,1:T(1,128)S(1)}, u32[]{:S(2)}, u32[]{:S(2)}) async-start(s32[1,32,128]{2,0,1:T(1,128)} %bitcast.12), calls=%async_computation.1 | async-start | bytes 32768 | tf_op jit(solution)/shard_map/all_to_all | solution.py:51
  65.1 0.3 copy.28
  65.4 0.3 stack.12
  65.7 0.3 stack.13
  66.1 0.3 stack.14
  66.4 0.7 pad_maximum_fusion
  67.1 12.1 %gather_fusion = bf16[4096,67]{1,0:T(8,128)(2,1)S(1)} fusion(bf16[67,2048]{0,1:T(8,128)(2,1)S(1)} %pad_maximum_fusion, s32[4096]{0:T(1024)S(1)} %fusion.19), kind=kCustom, calls=%fused_computation | custom fusion | bytes 1114112 | tf_op jit(solution)/shard_map/jit(_take)/gather | solution.py:47
  79.2 0.6 copy.32
  79.8 0.9 select_select_fusion
  80.8 9.2 %all-to-all-start = ((bf16[67,32,128]{2,0,1:T(8,128)(2,1)}), bf16[67,32,128]{2,0,1:T(8,128)(2,1)S(1)}, u32[]{:S(2)}, u32[]{:S(2)}) async-start(bf16[67,32,128]{2,0,1:T(8,128)(2,1)} %select_select_fusion), calls=%async_computation | async-start | bytes 1179648 | tf_op jit(solution)/shard_map/all_to_all | solution.py:50
  90.0 0.9 iota_compare_fusion.7
  90.9 15.6 %all-to-all-done = bf16[67,32,128]{2,0,1:T(8,128)(2,1)S(1)} async-done(((bf16[67,32,128]{2,0,1:T(8,128)(2,1)}), bf16[67,32,128]{2,0,1:T(8,128)(2,1)S(1)}, u32[]{:S(2)}, u32[]{:S(2)}) %all-to-all-start) | async-done | bytes 548896 | tf_op jit(solution)/shard_map/all_to_all | solution.py:50
  106.6 13.2 %fusion.9 = bf16[1536,128]{1,0:T(8,128)(2,1)S(1)} fusion(bf16[64,1536]{1,0:T(8,128)(2,1)S(1)} %copy-done, f32[4096]{0:T(1024)S(1)} %get-tuple-element.3, f32[4096]{0:T(1024)S(1)} %get-tuple-element.4, f32[4096]{0:T(1024)S(1)} %get-tuple-element.2, bf16[67,32,128]{2,0,1:T(8,128)(2,1)S(1)} %all-to-all-done, pred[4096,128]{1,0:T(32,128)(4,1)S(1)} %iota_compare_fusion.7), kind=kOutput, calls=%fused_computation.16 | convolution fusion | flops 2447769600 | bytes 1687552 | tf_op jit(solution)/shard_map/dot_general | solution.py:59
  119.8 0.2 copy.35
  120.0 6.0 %stack.11 = bf16[32,1536,128]{1,2,0:T(8,128)(2,1)} broadcast(bf16[1536,128]{0,1:T(8,128)(2,1)S(1)} %copy.35), dimensions={1,2} | broadcast | bytes 12976128 | tf_op jit(solution)/shard_map/stack | solution.py:62
  126.0 279.1 %all_to_all.25 = bf16[32,1536,128]{1,2,0:T(8,128)(2,1)S(1)} all-to-all(bf16[32,1536,128]{1,2,0:T(8,128)(2,1)} %stack.11), channel_id=1, replica_groups=mesh['paths'=8,'cpty'=32] {'cpty'}, dimensions={0} | all-to-all | bytes 25165824 | tf_op jit(solution)/shard_map/all_to_all | solution.py:62
  405.1 3.6 convolution_convert_fusion
  408.8 22.4 %all_to_all.26 = bf16[8,512,128]{2,1,0:T(8,128)(2,1)S(1)} all-to-all(bf16[8,512,128]{2,1,0:T(8,128)(2,1)S(1)} %bitcast.90), channel_id=1, replica_groups=mesh['paths'=8,'cpty'=32] {'paths'}, dimensions={0} | all-to-all | bytes 2097152 | tf_op jit(solution)/shard_map/all_to_all | solution.py:16
  431.1 0.1 convert_reduce_fusion
  431.3 0.7 broadcast_multiply_fusion
  (24 shorter events, 0.1 us)
Async XLA Ops:
  0.6 105.9 %copy-start = (bf16[64,1536]{1,0:T(8,128)(2,1)S(1)}, bf16[64,1536]{1,0:T(8,128)(2,1)}, u32[]{:S(2)}) copy-start(bf16[64,1536]{1,0:T(8,128)(2,1)} %param.6) | copy-start | bytes 589828
  0.6 19.6 %copy-start.1 = (s32[2048]{0:T(1024)S(1)}, s32[2048]{0:T(1024)}, u32[]{:S(2)}) copy-start(s32[2048]{0:T(1024)} %param.11) | copy-start | bytes 24580
  0.7 64.4 %copy-start.3 = (bf16[64,2048]{1,0:T(8,128)(2,1)S(1)}, bf16[64,2048]{1,0:T(8,128)(2,1)}, u32[]{:S(2)}) copy-start(bf16[64,2048]{1,0:T(8,128)(2,1)} %param.7) | copy-start | bytes 786436
  0.7 64.7 %copy-start.4 = (bf16[2048]{0:T(1024)(128)(2,1)S(1)}, bf16[2048]{0:T(1024)(128)(2,1)}, u32[]{:S(2)}) copy-start(bf16[2048]{0:T(1024)(128)(2,1)} %param.8) | copy-start | bytes 12292
  0.7 65.0 %copy-start.5 = (bf16[2048]{0:T(1024)(128)(2,1)S(1)}, bf16[2048]{0:T(1024)(128)(2,1)}, u32[]{:S(2)}) copy-start(bf16[2048]{0:T(1024)(128)(2,1)} %param.9) | copy-start | bytes 12292
  0.7 65.4 %copy-start.6 = (bf16[2048]{0:T(1024)(128)(2,1)S(1)}, bf16[2048]{0:T(1024)(128)(2,1)}, u32[]{:S(2)}) copy-start(bf16[2048]{0:T(1024)(128)(2,1)} %param.10) | copy-start | bytes 12292
  53.0 27.7 %all-to-all-start.1 = ((s32[1,32,128]{2,0,1:T(1,128)}), s32[1,32,128]{2,0,1:T(1,128)S(1)}, u32[]{:S(2)}, u32[]{:S(2)}) async-start(s32[1,32,128]{2,0,1:T(1,128)} %bitcast.12), calls=%async_computation.1 | async-start | bytes 32768 | tf_op jit(solution)/shard_map/all_to_all | solution.py:51
  80.8 25.8 %all-to-all-start = ((bf16[67,32,128]{2,0,1:T(8,128)(2,1)}), bf16[67,32,128]{2,0,1:T(8,128)(2,1)S(1)}, u32[]{:S(2)}, u32[]{:S(2)}) async-start(bf16[67,32,128]{2,0,1:T(8,128)(2,1)} %select_select_fusion), calls=%async_computation | async-start | bytes 1179648 | tf_op jit(solution)/shard_map/all_to_all | solution.py:50
  119.8 285.3 %copy-start.2 = (bf16[1536,128]{1,0:T(8,128)(2,1)}, bf16[1536,128]{1,0:T(8,128)(2,1)S(1)}, u32[]{:S(2)}) copy-start(bf16[1536,128]{1,0:T(8,128)(2,1)S(1)} %fusion.9) | copy-start | bytes 1179652
